TPU v7x, 32 devices: a whole 2x2x4 slice. The times are simulated.
32 devices in a mesh: sub: 8 (over z, y), grp: 4 (over x, core).
Axes of the slice: x: 2, y: 2, z: 4, core: 2. Of those that a mesh axis runs over, the one named last changes fastest.
Arguments:
- rr_inverse: float32 [64, 512, 512], P(('sub', 'grp')), may hold values from -4 to 4, as said below
- corner_modes: float32 [64, 64, 512], P(('sub', 'grp')), may hold values from -0.5 to 0.5
- coarse_inverse: float32 [2048, 2048], P(('sub', 'grp')), may hold values from -1 to 1, as said below
- inertia: float32 [64, 512], P(('sub', 'grp')), may hold values from 0.5 to 2
- disp_now: float32 [8, 64, 512], P(None, ('sub', 'grp')), may hold values from -4 to 4
- vel_now: float32 [8, 64, 512], P(None, ('sub', 'grp')), may hold values from -4 to 4
- acc_now: float32 [8, 64, 512], P(None, ('sub', 'grp')), may hold values from -8 to 8
- load_next: float32 [8, 64, 512], P(None, ('sub', 'grp')), may hold values from -10 to 10
- basis_rows: float32 [32768, 256], P(('sub', 'grp')), may hold values from -0.03125 to 0.03125
- piece_owner: int32 [32], replicated, may hold values from 0 to 31, each once
Outputs:
- disp_new: float32 [8, 64, 512], P(None, ('sub', 'grp'))
- vel_new: float32 [8, 64, 512], P(None, ('sub', 'grp'))
- projection: float32 [256, 8], replicated
- r_factor: float32 [8, 8], replicated
- new_columns: float32 [8, 32768], P(None, ('sub', 'grp'))
Inputs may be any that keep to these rules, and one draw needn't show every extreme that they name: piece_owner is a permutation. `rr_inverse`: each of the 64 blocks is symmetric positive definite. `coarse_inverse`: symmetric positive definite.
All inputs are finite; a program needn't handle non-finite values.
Results may differ from a plain program's by a relative error of at most 0.00018.
Values sent between devices are 32-bit elements; how exact they have to be, the bound alone decides.
A program may use at most 64 MiB of HBM per device.

v0:
```python
import math

import jax
import jax.numpy as jnp
from jax import lax
from jax.sharding import PartitionSpec as P

NC = 32
ITERS = 2
NI = 128


highest = lax.Precision.HIGHEST
time_step = 0.5
newmark_beta = 0.25
newmark_gamma = 0.5


def shifted(array, axis, by):
    count = lax.axis_size(axis)
    return lax.ppermute(array, axis, [(i, (i + by) % count) for i in range(count)])


def contract(segment, matrix_rows):
    return lax.dot_general(segment, matrix_rows, (((1,), (1,)), ((), ())), precision=highest)


def shards(
    rr_inverse,
    corner_modes,
    coarse_inverse,
    inertia,
    disp_now,
    vel_now,
    acc_now,
    load_next,
    basis_rows,
    piece_owner,
):
    case_count, sub_count, unknowns = disp_now.shape
    coarse_total = coarse_inverse.shape[1]
    row_count = sub_count * NC
    shifted_rows = jnp.roll(coarse_inverse, NC, axis=1)
    coarse_pairs = jnp.concatenate(
        [
            shifted_rows.reshape(row_count, coarse_total // NC, NC),
            coarse_inverse.reshape(row_count, coarse_total // NC, NC),
        ],
        axis=2,
    ).reshape(row_count, 2 * coarse_total)

    def apply_green(field):
        local_part = jnp.einsum("jab,cjb->cja", rr_inverse, field, precision=highest)
        corner_terms = jnp.einsum("jmb,cjb->cjm", corner_modes, field, precision=highest)
        flat_terms = corner_terms.reshape(case_count, sub_count * 2 * NC)
        owned_sums = contract(
            lax.all_gather(flat_terms, ("sub", "grp"), axis=1, tiled=True), coarse_pairs
        )
        previous = shifted(owned_sums[:, row_count - NC :], ("sub", "grp"), 1)
        owned_blocks = owned_sums.reshape(case_count, sub_count, NC)
        left_values = jnp.concatenate(
            [previous.reshape(case_count, 1, NC), owned_blocks[:, :-1]], axis=1
        )
        coarse_values = jnp.concatenate([left_values, owned_blocks], axis=2)
        return local_part + jnp.einsum(
            "jmb,cjm->cjb", corner_modes, coarse_values, precision=highest
        )

    def interface_jump(field):
        following = shifted(field[:, :1, :NI], ("sub", "grp"), -1)
        first_parts = jnp.concatenate([field[:, 1:, :NI], following], axis=1)
        return field[:, :, unknowns - NI :] - first_parts

    def squared_norm(values):
        return lax.psum(jnp.sum(values * values, axis=(1, 2)), ("sub", "grp"))

    right_side = load_next + inertia[None] * (
        disp_now + time_step * vel_now + (0.5 - newmark_beta) * time_step * time_step * acc_now
    )
    green_rhs = apply_green(right_side)
    residual = interface_jump(green_rhs)
    carried = green_rhs
    direction = residual
    norm_now = squared_norm(residual)
    for iteration in range(ITERS):
        earlier = shifted(direction[:, -1:], ("sub", "grp"), 1)
        left_parts = jnp.concatenate([earlier, direction[:, :-1]], axis=1)
        middle = jnp.zeros((case_count, sub_count, unknowns - 2 * NI), jnp.float32)
        image_field = apply_green(jnp.concatenate([-left_parts, middle, direction], axis=2))
        image = interface_jump(image_field)
        curvature = lax.psum(jnp.sum(direction * image, axis=(1, 2)), ("sub", "grp"))
        alpha = (norm_now / curvature)[:, None, None]
        carried = carried - alpha * image_field
        residual = residual - alpha * image
        if iteration + 1 < ITERS:
            norm_next = squared_norm(residual)
            direction = residual + (norm_next / norm_now)[:, None, None] * direction
            norm_now = norm_next
    accel_new = (
        (carried - disp_now) / (newmark_beta * time_step * time_step)
        - vel_now / (newmark_beta * time_step)
        - (0.5 / newmark_beta - 1.0) * acc_now
    )
    vel_new = vel_now + time_step * ((1.0 - newmark_gamma) * acc_now + newmark_gamma * accel_new)
    piece_total = lax.axis_size(("sub", "grp"))
    piece_rows = unknowns // piece_total
    inverse = (
        jnp.zeros((piece_total,), jnp.int32)
        .at[piece_owner]
        .set(jnp.arange(piece_total, dtype=jnp.int32))
    )
    outgoing = carried.reshape(case_count, sub_count, piece_total, piece_rows)[:, :, inverse, :]
    outgoing = jnp.transpose(outgoing, (0, 2, 1, 3)).reshape(
        case_count, piece_total * sub_count * piece_rows
    )
    received = lax.all_to_all(outgoing, ("sub", "grp"), split_axis=1, concat_axis=1, tiled=True)
    projection_part = lax.dot_general(
        basis_rows, received, (((0,), (1,)), ((), ())), precision=highest
    )
    projection = lax.psum(projection_part, ("sub", "grp"))
    remainder = received - lax.dot_general(
        projection, basis_rows, (((0,), (1,)), ((), ())), precision=highest
    )
    gram_local = lax.dot_general(remainder, remainder, (((1,), (1,)), ((), ())), precision=highest)
    lower = jnp.linalg.cholesky(lax.psum(gram_local, ("sub", "grp")))
    scale_rows = math.sqrt(received.shape[1] * piece_total)
    new_columns = jax.scipy.linalg.solve_triangular(lower, remainder, lower=True) * scale_rows
    r_factor = lower.T / scale_rows
    return (carried, vel_new, projection, r_factor, new_columns)


def solution(mesh):
    return jax.shard_map(
        shards,
        mesh=mesh,
        in_specs=(
            P(("sub", "grp"), None, None),
            P(("sub", "grp"), None, None),
            P(("sub", "grp"), None),
            P(("sub", "grp"), None),
            P(None, ("sub", "grp"), None),
            P(None, ("sub", "grp"), None),
            P(None, ("sub", "grp"), None),
            P(None, ("sub", "grp"), None),
            P(("sub", "grp"), None),
            P(),
        ),
        out_specs=(
            P(None, ("sub", "grp"), None),
            P(None, ("sub", "grp"), None),
            P(),
            P(),
            P(None, ("sub", "grp")),
        ),
        check_vma=False,
    )
```

profile of v0, /device:TPU:0, one launch (start us, length us, event | category | flops | bytes accessed | tf_op | source)
XLA Modules:
  0.0 396.2 jit_solution(17063526511338648422)
XLA Ops:
  0.7 1.5 copy.65
  3.8 43.6 %all_gather.9 = f32[8,4096]{1,0:T(8,128)S(1)} all-gather(f32[8,128]{1,0:T(8,128)S(1)} %reshape.67), channel_id=1, replica_groups=mesh['sub'=8,'grp'=4] {'sub','grp'}, dimensions={1}, use_global_device_ids=true | all-gather | bytes 135168 | tf_op jit(solution)/shard_map/all_gather | solution.py:57
  51.8 1.8 fusion.10
  53.7 4.4 %collective-permute-done = f32[8,32]{1,0:T(8,128)S(1)} collective-permute-done((f32[8,32]{1,0:T(8,128)S(1)}, f32[8,32]{1,0:T(8,128)S(1)}, u32[]{:S(2)}, u32[]{:S(2)}) %collective-permute-start) | collective-permute-done | bytes 1056 | tf_op jit(solution)/shard_map/ppermute | solution.py:21
  60.4 6.6 %collective-permute-done.2 = f32[8,1,128]{2,0,1:T(8,128)S(1)} collective-permute-done((f32[8,1,128]{2,0,1:T(8,128)S(1)}, f32[8,1,128]{2,0,1:T(8,128)S(1)}, u32[]{:S(2)}, u32[]{:S(2)}) %collective-permute-start.2) | collective-permute-done | bytes 4128 | tf_op jit(solution)/shard_map/ppermute | solution.py:21
  67.4 36.7 %all_gather.10 = f32[8,4096]{1,0:T(8,128)S(1)} all-gather(f32[8,128]{1,0:T(8,128)S(1)} %reshape.73), channel_id=1, replica_groups=mesh['sub'=8,'grp'=4] {'sub','grp'}, dimensions={1}, use_global_device_ids=true | all-gather | bytes 135168 | tf_op jit(solution)/shard_map/all_gather | solution.py:57
  104.1 2.7 fusion.50
  107.2 1.8 fusion.5
  109.1 4.4 %collective-permute-done.3 = f32[8,32]{1,0:T(8,128)S(1)} collective-permute-done((f32[8,32]{1,0:T(8,128)S(1)}, f32[8,32]{1,0:T(8,128)S(1)}, u32[]{:S(2)}, u32[]{:S(2)}) %collective-permute-start.3) | collective-permute-done | bytes 1056 | tf_op jit(solution)/shard_map/ppermute | solution.py:21
  116.0 38.1 %all-reduce = (f32[8]{0:T(128)S(1)}, f32[8]{0:T(128)S(1)}) all-reduce(f32[8]{0:T(128)S(1)} %get-tuple-element.21, f32[8]{0:T(128)S(1)} %get-tuple-element.20), channel_id=1, replica_groups=mesh['sub'=8,'grp'=4] {'sub','grp'}, use_global_device_ids=true, to_apply=%region_1.2 | all-reduce | flops 16 | bytes 128 | tf_op jit(solution)/shard_map/psum | solution.py:75
  154.3 42.1 %psum.44 = f32[8]{0:T(128)S(1)} all-reduce(f32[8]{0:T(128)S(1)} %multiply_reduce_fusion), channel_id=1, replica_groups=mesh['sub'=8,'grp'=4] {'sub','grp'}, use_global_device_ids=true, to_apply=%region_5.6 | all-reduce | flops 8 | bytes 64 | tf_op jit(solution)/shard_map/psum | solution.py:75
  197.2 5.9 %collective-permute-done.5 = f32[8,1,128]{2,0,1:T(8,128)S(1)} collective-permute-done((f32[8,1,128]{2,0,1:T(8,128)S(1)}, f32[8,1,128]{2,0,1:T(8,128)S(1)}, u32[]{:S(2)}, u32[]{:S(2)}) %collective-permute-start.5) | collective-permute-done | bytes 4128 | tf_op jit(solution)/shard_map/ppermute | solution.py:21
  203.5 36.7 %all_gather.11 = f32[8,4096]{1,0:T(8,128)S(1)} all-gather(f32[8,128]{1,0:T(8,128)S(1)} %reshape.76), channel_id=1, replica_groups=mesh['sub'=8,'grp'=4] {'sub','grp'}, dimensions={1}, use_global_device_ids=true | all-gather | bytes 135168 | tf_op jit(solution)/shard_map/all_gather | solution.py:57
  240.2 2.7 fusion.51
  243.4 2.5 fusion.6
  246.0 3.7 collective-permute-done.6
  253.6 38.1 %psum.45 = f32[8]{0:T(128)S(1)} all-reduce(f32[8]{0:T(128)S(1)} %fusion.17), channel_id=1, replica_groups=mesh['sub'=8,'grp'=4] {'sub','grp'}, use_global_device_ids=true, to_apply=%region_7.8 | all-reduce | flops 8 | bytes 64 | tf_op jit(solution)/shard_map/psum | solution.py:91
  291.7 1.5 fusion.4
  294.2 1.5 gather_fusion
  296.7 6.5 %all-to-all-start = ((f32[32,1,256]{2,1,0:T(1,128)}), f32[32,1,256]{2,1,0:T(1,128)S(1)}, u32[]{:S(2)}, u32[]{:S(2)}) async-start(f32[32,1,256]{2,1,0:T(1,128)} %reshape.100), calls=%async_computation | async-start | bytes 65536 | tf_op jit(solution)/shard_map/all_to_all | solution.py:116
  303.2 1.4 copy.88
  306.0 4.5 %all-to-all-done = f32[32,1,256]{2,1,0:T(1,128)S(1)} async-done(((f32[32,1,256]{2,1,0:T(1,128)}), f32[32,1,256]{2,1,0:T(1,128)S(1)}, u32[]{:S(2)}, u32[]{:S(2)}) %all-to-all-start) | async-done | bytes 32800 | tf_op jit(solution)/shard_map/all_to_all | solution.py:116
  312.5 38.3 %psum.46 = f32[256,8]{0,1:T(8,128)S(1)} all-reduce(f32[256,8]{0,1:T(8,128)S(1)} %convolution_bitcast_fusion), channel_id=1, replica_groups=mesh['sub'=8,'grp'=4] {'sub','grp'}, use_global_device_ids=true, to_apply=%region_9.10 | all-reduce | flops 2048 | bytes 16384 | tf_op jit(solution)/shard_map/psum | solution.py:120
  351.8 40.1 %psum.47 = f32[8,8]{0,1:T(8,128)S(1)} all-reduce(f32[8,8]{0,1:T(8,128)S(1)} %fusion.52), channel_id=1, replica_groups=mesh['sub'=8,'grp'=4] {'sub','grp'}, use_global_device_ids=true, to_apply=%region_10.11 | all-reduce | flops 64 | bytes 512 | tf_op jit(solution)/shard_map/psum | solution.py:125
  (110 shorter events, 28.4 us)
Async XLA Ops:
  0.6 51.1 %copy-start = (f32[2,512,512]{2,1,0:T(8,128)S(1)}, f32[2,512,512]{2,1,0:T(8,128)}, u32[]{:S(2)}) copy-start(f32[2,512,512]{2,1,0:T(8,128)} %param.10) | copy-start | bytes 6291460
  0.6 2.7 copy-start.6
  0.7 2.7 copy-start.7
  0.7 2.6 copy-start.5
  0.7 2.7 copy-start.2
  2.2 1.1 copy-start.9
  2.2 1.1 copy-start.10
  48.9 1.4 copy-start.1
  51.4 6.7 %collective-permute-start = (f32[8,32]{1,0:T(8,128)S(1)}, f32[8,32]{1,0:T(8,128)S(1)}, u32[]{:S(2)}, u32[]{:S(2)}) collective-permute-start(f32[8,32]{1,0:T(8,128)S(1)} %slice.79), channel_id=1, source_target_pairs={{0,1},{1,2},{2,3},{3,4},{4,5},{5,6},{6,7},{7,8},{8,9},{9,10},{10,1... | collective-permute-start | bytes 3080 | tf_op jit(solution)/shard_map/ppermute | solution.py:21
  58.4 2.0 collective-permute-start.1
  60.4 6.6 %collective-permute-start.2 = (f32[8,1,128]{2,0,1:T(8,128)S(1)}, f32[8,1,128]{2,0,1:T(8,128)S(1)}, u32[]{:S(2)}, u32[]{:S(2)}) collective-permute-start(f32[8,1,128]{2,0,1:T(8,128)S(1)} %get-tuple-element.34), channel_id=1, source_target_pairs={{0,1},{1,2},{2,3},{3,4},{4,5},{5,6},{6,7},{7,8},{8,9},{9,10},{10,1... | collective-permute-start | bytes 12296 | tf_op jit(solution)/shard_map/ppermute | solution.py:21
  104.1 92.4 %copy-start.11 = (s32[32]{0:T(128)S(1)}, s32[32]{0:T(128)}, u32[]{:S(2)}) copy-start(s32[32]{0:T(128)} %param.19) | copy-start | bytes 388
  106.9 6.6 %collective-permute-start.3 = (f32[8,32]{1,0:T(8,128)S(1)}, f32[8,32]{1,0:T(8,128)S(1)}, u32[]{:S(2)}, u32[]{:S(2)}) collective-permute-start(f32[8,32]{1,0:T(8,128)S(1)} %slice.86), channel_id=1, source_target_pairs={{0,1},{1,2},{2,3},{3,4},{4,5},{5,6},{6,7},{7,8},{8,9},{9,10},{10,1... | collective-permute-start | bytes 3080 | tf_op jit(solution)/shard_map/ppermute | solution.py:21
  113.8 2.0 collective-permute-start.4
  196.4 6.6 %collective-permute-start.5 = (f32[8,1,128]{2,0,1:T(8,128)S(1)}, f32[8,1,128]{2,0,1:T(8,128)S(1)}, u32[]{:S(2)}, u32[]{:S(2)}) collective-permute-start(f32[8,1,128]{2,0,1:T(8,128)S(1)} %get-tuple-element.32), channel_id=1, source_target_pairs={{0,1},{1,2},{2,3},{3,4},{4,5},{5,6},{6,7},{7,8},{8,9},{9,10},{10,1... | collective-permute-start | bytes 12296 | tf_op jit(solution)/shard_map/ppermute | solution.py:21
  242.9 6.8 %collective-permute-start.6 = (f32[8,32]{1,0:T(8,128)S(1)}, f32[8,32]{1,0:T(8,128)S(1)}, u32[]{:S(2)}, u32[]{:S(2)}) collective-permute-start(f32[8,32]{1,0:T(8,128)S(1)} %slice.93), channel_id=1, source_target_pairs={{0,1},{1,2},{2,3},{3,4},{4,5},{5,6},{6,7},{7,8},{8,9},{9,10},{10,1... | collective-permute-start | bytes 3080 | tf_op jit(solution)/shard_map/ppermute | solution.py:21
  245.9 66.0 %copy-start.3 = (f32[1024,256]{1,0:T(8,128)S(1)}, f32[1024,256]{1,0:T(8,128)}, u32[]{:S(2)}) copy-start(f32[1024,256]{1,0:T(8,128)} %param.18) | copy-start | bytes 3145732
  250.8 2.7 collective-permute-start.7
  293.2 2.5 copy-start.4
  296.7 13.7 %all-to-all-start = ((f32[32,1,256]{2,1,0:T(1,128)}), f32[32,1,256]{2,1,0:T(1,128)S(1)}, u32[]{:S(2)}, u32[]{:S(2)}) async-start(f32[32,1,256]{2,1,0:T(1,128)} %reshape.100), calls=%async_computation | async-start | bytes 65536 | tf_op jit(solution)/shard_map/all_to_all | solution.py:116
  350.7 45.5 %copy-start.8 = (f32[256,8]{0,1:T(8,128)}, f32[256,8]{0,1:T(8,128)S(1)}, u32[]{:S(2)}) copy-start(f32[256,8]{0,1:T(8,128)S(1)} %psum.46) | copy-start | bytes 24580
where the time goes:
time: 397 us; the launch traced here: 396 us
  blocking collectives  314 us (79%)
  waiting for transfers between devices  33.4 us (8%)
  matrix products  17.6 us (4%)
  local copies, waits for them, and re-layouts  13.2 us (3%)
  starting transfers between devices  10.5 us (3%)
  other arithmetic  6.97 us (2%)
    all_gather x3, blocking collectives, apply_green(): lax.all_gather(flat_terms, ('sub', 'grp'), axis=1, tiled=True)  117 us
    psum x2, blocking collectives, squared_norm(): return lax.psum(jnp.sum(values * values, axis=(1, 2)), ('sub', 'grp'))  80.2 us
    psum x1, blocking collectives, shards(): lower = jnp.linalg.cholesky(lax.psum(gram_local, ('sub', 'grp')))  40.1 us
    psum x1, blocking collectives, shards(): projection = lax.psum(projection_part, ('sub', 'grp'))  38.3 us
    psum x1, blocking collectives, shards(): lax.psum(jnp.sum(direction * image, axis=(1, 2)), ('sub', 'grp'))  38.1 us
    ppermute x8, waiting for transfers between devices, shifted(): lax.ppermute(array, axis, [(i, (i + by) % count) for i in range(count)])  29 us
  transfers between devices with their start and end apart: 9, of which 9 were waited for; matrix products, arithmetic and copies ran while one was open for 2% of the time, Pallas kernels for 0%

commit v1 on v0

v1 whole, which is shorter than its diff:
```python
import functools
import math

import jax
import jax.numpy as jnp
from jax import lax
from jax.experimental import pallas as pl
from jax.experimental.pallas import tpu as pltpu
from jax.sharding import PartitionSpec as P

NC = 32
NI = 128
LANES = 128

time_step = 0.5
newmark_beta = 0.25
newmark_gamma = 0.5

MESH = pl.DeviceIdType.MESH


def nn(a, b):
    return lax.dot_general(
        a, b, (((1,), (0,)), ((), ())), precision=lax.Precision.HIGHEST, preferred_element_type=jnp.float32
    )


def nt(a, b):
    return lax.dot_general(
        a, b, (((1,), (1,)), ((), ())), precision=lax.Precision.HIGHEST, preferred_element_type=jnp.float32
    )


def kernel(
    n,
    groups,
    inverse,
    rr_hbm,
    modes_hbm,
    coarse_hbm,
    basis_hbm,
    inertia,
    disp_now,
    vel_now,
    acc_now,
    load_next,
    disp_out,
    vel_out,
    proj_out,
    r_out,
    cols_out,
    rr,
    modes,
    coarse,
    basis,
    modes_next,
    rr_next,
    corner,
    inter,
    gathered,
    edge,
    edge_out,
    norms,
    pieces,
    outgoing,
    incoming,
    proj_parts,
    gram_parts,
    green,
    local_sem,
    const_send,
    const_recv,
    wide_send,
    wide_recv,
    edge_send,
    edge_recv,
):
    sub_count, unknowns = rr.shape[0], rr.shape[1]
    rows = sub_count * NC
    me = lax.axis_index("sub") * groups + lax.axis_index("grp")
    following = lax.rem(me + 1, n)
    earlier = lax.rem(me + n - 1, n)

    def device(rank):
        return (rank // groups, lax.rem(rank, groups))

    def others(body):
        def step(i, carry):
            body(lax.rem(me + i, n))
            return carry

        lax.fori_loop(1, n, step, 0)

    def remote(src, dst, send, recv, rank):
        return pltpu.make_async_remote_copy(
            src_ref=src, dst_ref=dst, send_sem=send, recv_sem=recv, device_id=device(rank), device_id_type=MESH
        )

    barrier = pltpu.get_barrier_semaphore()
    others(lambda rank: pl.semaphore_signal(barrier, inc=1, device_id=device(rank), device_id_type=MESH))

    load_rr = pltpu.make_async_copy(rr_hbm, rr, local_sem.at[0])
    load_modes = pltpu.make_async_copy(modes_hbm, modes, local_sem.at[1])
    load_coarse = pltpu.make_async_copy(coarse_hbm, coarse.at[pl.ds(0, rows)], local_sem.at[2])
    load_basis = pltpu.make_async_copy(basis_hbm, basis, local_sem.at[3])
    load_modes.start()
    load_rr.start()
    load_coarse.start()
    load_basis.start()

    lane = lax.broadcasted_iota(jnp.int32, (8, LANES), 1)
    sublane = lax.broadcasted_iota(jnp.int32, (8, LANES), 0)

    def right_side(k):
        return load_next[:, k, :] + inertia[k : k + 1, :] * (
            disp_now[:, k, :]
            + time_step * vel_now[:, k, :]
            + (0.5 - newmark_beta) * time_step * time_step * acc_now[:, k, :]
        )

    sides = [right_side(k) for k in range(sub_count)]

    corner[...] = jnp.zeros_like(corner)
    load_modes.wait()
    corner[0:NC, 0:unknowns] = modes[0, NC:, :]
    corner[0:NC, unknowns:] = modes[1, :NC, :]
    corner[NC : 2 * NC, unknowns:] = modes[1, NC:, :]
    corner[3 * NC :, 0:unknowns] = modes[0, :NC, :]

    odd = lax.rem(me, 2) == 1

    def placed(tile):
        return jnp.where(odd, pltpu.roll(tile, 64, 1), tile)

    def broadcast(buffer, at, sem):
        def send(rank):
            remote(buffer.at[at, me], buffer.at[at, me], wide_send.at[sem], wide_recv.at[sem], rank).start()

        others(send)

    def all_but_one(buffer, at, sem):
        return pltpu.make_async_copy(buffer.at[at, pl.ds(0, n - 1)], buffer.at[at, pl.ds(0, n - 1)], sem)

    gathered[0, me] = placed(nt(jnp.concatenate(sides, axis=1), corner[...]))

    pl.semaphore_wait(barrier, n - 1)
    broadcast(gathered, 0, 0)

    constants = [
        remote(coarse_hbm.at[pl.ds(0, NC)], coarse.at[pl.ds(rows, NC)], const_send.at[0], const_recv.at[0], earlier),
        remote(
            coarse_hbm.at[pl.ds(rows - NC, NC)],
            coarse.at[pl.ds(rows + NC, NC)],
            const_send.at[1],
            const_recv.at[1],
            following,
        ),
        remote(modes_hbm.at[0, :, pl.ds(0, NI)], modes_next, const_send.at[2], const_recv.at[2], earlier),
        remote(
            rr_hbm.at[0, pl.ds(0, NI), pl.ds(0, NI)],
            rr_next.at[pl.ds(0, NI)],
            const_send.at[3],
            const_recv.at[3],
            earlier,
        ),
        remote(
            rr_hbm.at[0, pl.ds(unknowns - NI, NI), pl.ds(0, NI)],
            rr_next.at[pl.ds(NI, NI)],
            const_send.at[4],
            const_recv.at[4],
            earlier,
        ),
    ]
    for copy in constants:
        copy.start()

    load_rr.wait()
    local = [nn(sides[k], rr[k]) for k in range(sub_count)]
    edge_out[0] = local[0][:, :NI]
    edges = [remote(edge_out.at[0], edge.at[0], edge_send.at[0], edge_recv.at[0], earlier)]
    edges[0].start()

    load_coarse.wait()
    for copy in constants:
        copy.wait_recv()
    inter[...] = jnp.zeros_like(inter)
    inter[0:NC, 0:NI] = modes[0, NC:, unknowns - NI :] - modes[1, :NC, :NI]
    inter[0:NC, NI:] = modes[1, :NC, unknowns - NI :]
    inter[NC : 2 * NC, 0:NI] = -modes[1, NC:, :NI]
    inter[NC : 2 * NC, NI:] = modes[1, NC:, unknowns - NI :] - modes_next[:NC, :]
    inter[2 * NC : 3 * NC, NI:] = -modes_next[NC:, :]
    inter[3 * NC :, 0:NI] = modes[0, :NC, unknowns - NI :]

    def coarse_solve(at):
        all_but_one(gathered, at, wide_recv.at[at]).wait()
        assembled = []
        for j in range(n // 2):
            low = jnp.where(lane < 96, gathered[at, 2 * j], gathered[at, (2 * j + 2) % n])
            high = jnp.where(lane >= 32, gathered[at, 2 * j + 1], gathered[at, (2 * j - 1) % n])
            assembled.append(low + high)
        return nt(jnp.concatenate(assembled, axis=1), coarse[...])

    def jumps(fields, next_first):
        firsts = [field[:, :NI] for field in fields[1:]] + [next_first]
        return jnp.concatenate(
            [field[:, unknowns - NI :] - first for field, first in zip(fields, firsts)], axis=1
        )

    per_piece = unknowns // n
    width = sub_count * per_piece

    def piece_part(fields, which, p):
        block = p * per_piece // LANES
        inside = p * per_piece % LANES
        part = jnp.zeros((8, LANES), jnp.float32)
        for k in range(sub_count):
            target = which * width + k * per_piece
            rolled = pltpu.roll(
                fields[k][:, block * LANES : (block + 1) * LANES], (target - inside) % LANES, 1
            )
            part = jnp.where((lane >= target) & (lane < target + per_piece), rolled, part)
        return part

    solved = coarse_solve(0)
    edges[0].wait_recv()
    first_fields = [
        local[k] + nn(solved, corner[:, k * unknowns : (k + 1) * unknowns]) for k in range(sub_count)
    ]
    vector0 = jumps(local, edge[0]) + nn(solved, inter[...])

    def start_image(vector, at):
        gathered[at, me] = placed(nt(vector, inter[...]))
        broadcast(gathered, at, at)
        slot = 2 * at - 1
        edge_out[slot] = vector[:, NI:]
        edge_out[slot + 1] = vector[:, :NI]
        for offset, rank in ((0, following), (1, earlier)):
            copy = remote(
                edge_out.at[slot + offset],
                edge.at[slot + offset],
                edge_send.at[slot + offset],
                edge_recv.at[slot + offset],
                rank,
            )
            copy.start()
            edges.append(copy)

    def end_image(vector, at):
        slot = 2 * at - 1
        head, tail = vector[:, :NI], vector[:, NI:]
        second = nn(-head, rr[1, :NI, :]) + nn(tail, rr[1, unknowns - NI :, :])
        edges[slot].wait_recv()
        edges[slot + 1].wait_recv()
        first = nn(-edge[slot], rr[0, :NI, :]) + nn(head, rr[0, unknowns - NI :, :])
        beyond = nn(-tail, rr_next[:NI, :]) + nn(edge[slot + 1], rr_next[NI:, :])
        inner = [first, second]
        values = coarse_solve(at)
        fields = [
            inner[k] + nn(values, corner[:, k * unknowns : (k + 1) * unknowns]) for k in range(sub_count)
        ]
        return fields, jumps(inner, beyond) + nn(values, inter[...])

    def column(values):
        return jnp.sum(values, axis=1, keepdims=True)

    start_image(vector0, 1)
    for k in range(sub_count):
        green[k] = first_fields[k]
    for p in range(n):
        pieces[p] = piece_part(first_fields, 0, p)
    fields0, vector1 = end_image(vector0, 1)

    start_image(vector1, 2)
    norm_row = jnp.where(lane == sublane, column(vector0 * vector0), 0.0) + jnp.where(
        lane == sublane + 8, column(vector0 * vector1), 0.0
    )
    norms[0, me] = jnp.sum(norm_row, axis=0, keepdims=True)
    broadcast(norms, 0, 3)
    for p in range(n):
        pieces[p] = pieces[p] + piece_part(fields0, 1, p)
    fields1, vector2 = end_image(vector1, 2)

    all_but_one(norms, 0, wide_recv.at[3]).wait()
    totals = jnp.broadcast_to(jnp.sum(norms[0], axis=0), (8, LANES))
    norm0 = column(jnp.where(lane == sublane, totals, 0.0))
    curve0 = column(jnp.where(lane == sublane + 8, totals, 0.0))
    alpha0 = norm0 / curve0
    residual = vector0 - alpha0 * vector1
    residual_image = vector1 - alpha0 * vector2
    extra = (
        jnp.where(lane == 3 * width, column(residual * residual), 0.0)
        + jnp.where(lane == 3 * width + 1, column(residual * residual_image), 0.0)
        + jnp.where(lane == 3 * width + 2, column(residual * vector1), 0.0)
    )
    for p in range(n):
        pieces[p] = pieces[p] + piece_part(fields1, 2, p) + extra
    for t in range(n):
        outgoing[t] = pieces[inverse[t]]

    def send_piece(rank):
        remote(outgoing.at[rank], incoming.at[0, me], wide_send.at[4], wide_recv.at[4], rank).start()

    others(send_piece)
    incoming[0, me] = outgoing[me]
    load_basis.wait()
    all_but_one(incoming, 0, wide_recv.at[4]).wait()

    sums = jnp.sum(incoming[0], axis=0)
    norm1 = column(jnp.where(lane == 3 * width, sums, 0.0))
    curve_rr = column(jnp.where(lane == 3 * width + 1, sums, 0.0))
    curve_rp = column(jnp.where(lane == 3 * width + 2, sums, 0.0))
    beta = norm1 / norm0
    curve1 = curve_rr + 2.0 * beta * curve_rp + beta * beta * curve0
    alpha1 = norm1 / curve1
    scale0 = alpha0 + alpha1 * (1.0 + beta)
    scale1 = -alpha1 * alpha0

    factor = jnp.where(lane < width, 1.0, jnp.where(lane < 2 * width, -scale0, -scale1))
    factor = jnp.where(lane < 3 * width, factor, 0.0)
    per_tile = LANES // width
    snapshot_tiles = []
    for j in range(n // per_tile):
        tile = jnp.zeros((8, LANES), jnp.float32)
        for i in range(per_tile):
            scaled = incoming[0, j * per_tile + i] * factor
            total = scaled
            for which in (1, 2):
                total = total + pltpu.roll(scaled, LANES - which * width, 1)
            if i:
                total = pltpu.roll(total, i * width, 1)
            tile = jnp.where((lane >= i * width) & (lane < (i + 1) * width), total, tile)
        snapshot_tiles.append(tile)
    snapshots = jnp.concatenate(snapshot_tiles, axis=1)
    proj_parts[0, me] = nn(snapshots, basis[...])
    broadcast(proj_parts, 0, 5)

    for k in range(sub_count):
        carried = green[k] - scale0 * fields0[k] - scale1 * fields1[k]
        now, vel, acc = disp_now[:, k, :], vel_now[:, k, :], acc_now[:, k, :]
        accel_new = (
            (carried - now) / (newmark_beta * time_step * time_step)
            - vel / (newmark_beta * time_step)
            - (0.5 / newmark_beta - 1.0) * acc
        )
        disp_out[:, k, :] = carried
        vel_out[:, k, :] = vel + time_step * ((1.0 - newmark_gamma) * acc + newmark_gamma * accel_new)

    all_but_one(proj_parts, 0, wide_recv.at[5]).wait()
    projection = jnp.sum(proj_parts[0], axis=0)
    proj_out[...] = projection
    remainder = snapshots - nt(projection, basis[...])
    repeated = jnp.concatenate([remainder] * (LANES // 8), axis=0)
    gram_wide = nt(remainder, repeated)
    gram_parts[0, me] = jnp.sum(
        jnp.where(lane // 8 == sublane, gram_wide, 0.0), axis=0, keepdims=True
    )
    broadcast(gram_parts, 0, 6)
    all_but_one(gram_parts, 0, wide_recv.at[6]).wait()
    gram_row = jnp.broadcast_to(jnp.sum(gram_parts[0], axis=0), (8, LANES))
    work = gram_row
    for i in range(1, 8):
        work = jnp.where(sublane == i, pltpu.roll(gram_row, LANES - 8 * i, 1), work)
    for j in range(8):
        inverse_root = lax.rsqrt(work[j : j + 1, j : j + 1])
        pivot = work[j : j + 1, :] * inverse_root
        below = work[:, j : j + 1] * inverse_root
        pivot_rows = remainder[j : j + 1, :] * inverse_root
        work = jnp.where(sublane == j, pivot, jnp.where(sublane > j, work - below * pivot, work))
        row_at = lax.broadcasted_iota(jnp.int32, remainder.shape, 0)
        remainder = jnp.where(
            row_at == j, pivot_rows, jnp.where(row_at > j, remainder - below * pivot_rows, remainder)
        )
    scale_rows = math.sqrt(snapshots.shape[1] * n)
    r_out[...] = jnp.where(lane >= sublane, work, 0.0)[:, :8] * (1.0 / scale_rows)
    cols_out[...] = remainder * scale_rows

    for copy in constants + edges:
        copy.wait_send()
    for at in range(3):
        all_but_one(gathered, at, wide_send.at[at]).wait()
    all_but_one(norms, 0, wide_send.at[3]).wait()
    all_but_one(incoming, 0, wide_send.at[4]).wait()
    all_but_one(proj_parts, 0, wide_send.at[5]).wait()
    all_but_one(gram_parts, 0, wide_send.at[6]).wait()


def solution(mesh):
    groups = mesh.shape["grp"]
    n = mesh.shape["sub"] * groups

    def shards(
        rr_inverse,
        corner_modes,
        coarse_inverse,
        inertia,
        disp_now,
        vel_now,
        acc_now,
        load_next,
        basis_rows,
        piece_owner,
    ):
        case_count, sub_count, unknowns = disp_now.shape
        rank = basis_rows.shape[1]
        local_rows = basis_rows.shape[0]
        counting = jnp.arange(n, dtype=jnp.int32)
        inverse = jnp.sum(
            jnp.where(piece_owner[None, :] == counting[:, None], counting[None, :], 0), axis=1, dtype=jnp.int32
        )
        width = (sub_count + 2) * NC
        f32 = jnp.float32
        vmem = pl.BlockSpec(memory_space=pltpu.VMEM)
        anywhere = pl.BlockSpec(memory_space=pl.ANY)
        disp, vel, proj, r_factor, columns = pl.pallas_call(
            functools.partial(kernel, n, groups),
            out_shape=(
                jax.ShapeDtypeStruct(disp_now.shape, f32),
                jax.ShapeDtypeStruct(disp_now.shape, f32),
                jax.ShapeDtypeStruct((case_count, rank), f32),
                jax.ShapeDtypeStruct((case_count, case_count), f32),
                jax.ShapeDtypeStruct((case_count, local_rows), f32),
            ),
            in_specs=[pl.BlockSpec(memory_space=pltpu.SMEM)] + [anywhere] * 4 + [vmem] * 5,
            out_specs=(vmem,) * 5,
            scratch_shapes=[
                pltpu.VMEM(rr_inverse.shape, f32),
                pltpu.VMEM(corner_modes.shape, f32),
                pltpu.VMEM((width, coarse_inverse.shape[1]), f32),
                pltpu.VMEM(basis_rows.shape, f32),
                pltpu.VMEM((2 * NC, NI), f32),
                pltpu.VMEM((2 * NI, NI), f32),
                pltpu.VMEM((width, sub_count * unknowns), f32),
                pltpu.VMEM((width, sub_count * NI), f32),
                pltpu.VMEM((3, n, case_count, width), f32),
                pltpu.VMEM((5, case_count, NI), f32),
                pltpu.VMEM((5, case_count, NI), f32),
                pltpu.VMEM((1, n, 1, LANES), f32),
                pltpu.VMEM((n, case_count, LANES), f32),
                pltpu.VMEM((n, case_count, LANES), f32),
                pltpu.VMEM((1, n, case_count, LANES), f32),
                pltpu.VMEM((1, n, case_count, rank), f32),
                pltpu.VMEM((1, n, 1, LANES), f32),
                pltpu.VMEM((sub_count, case_count, unknowns), f32),
                pltpu.SemaphoreType.DMA((4,)),
                pltpu.SemaphoreType.DMA((5,)),
                pltpu.SemaphoreType.DMA((5,)),
                pltpu.SemaphoreType.DMA((7,)),
                pltpu.SemaphoreType.DMA((7,)),
                pltpu.SemaphoreType.DMA((5,)),
                pltpu.SemaphoreType.DMA((5,)),
            ],
            compiler_params=pltpu.CompilerParams(collective_id=0, has_side_effects=True),
        )(
            inverse,
            rr_inverse,
            corner_modes,
            coarse_inverse,
            basis_rows,
            inertia,
            disp_now,
            vel_now,
            acc_now,
            load_next,
        )
        return disp, vel, proj.T, r_factor, columns

    return jax.shard_map(
        shards,
        mesh=mesh,
        in_specs=(
            P(("sub", "grp"), None, None),
            P(("sub", "grp"), None, None),
            P(("sub", "grp"), None),
            P(("sub", "grp"), None),
            P(None, ("sub", "grp"), None),
            P(None, ("sub", "grp"), None),
            P(None, ("sub", "grp"), None),
            P(None, ("sub", "grp"), None),
            P(("sub", "grp"), None),
            P(),
        ),
        out_specs=(
            P(None, ("sub", "grp"), None),
            P(None, ("sub", "grp"), None),
            P(),
            P(),
            P(None, ("sub", "grp")),
        ),
        check_vma=False,
    )
```

time: 397 us -> 69.5 us (0.18)
  blocking collectives: 314 us -> 0 us
  Pallas kernels: 0 us -> 60.4 us
  waiting for transfers between devices: 33.4 us -> 0 us
  matrix products: 17.6 us -> 0 us
  starting transfers between devices: 10.5 us -> 0 us
  local copies, waits for them, and re-layouts: 13.2 us -> 6.69 us
  other arithmetic: 6.97 us -> 1.28 us
    psum x5 -> x0, blocking collectives: 197 us -> none  [the longest x2 80.2 us: squared_norm(): return lax.psum(jnp.sum(values * values, axis=(1, 2)), ('sub', 'grp'))]
    all_gather x3 -> x0, blocking collectives: 117 us -> none  [apply_green(): lax.all_gather(flat_terms, ('sub', 'grp'), axis=1, tiled=True)]
    pallas_call x0 -> x1, Pallas kernels: none -> 60.4 us  [shards(): pl.pallas_call(functools.partial(kernel, n, groups), out_shape=(jax.Shape...]
    ppermute x8 -> x0, waiting for transfers between devices: 29 us -> none  [shifted(): lax.ppermute(array, axis, [(i, (i + by) % count) for i in range(count)])]
    dot_general x15 -> x0, matrix products: 16.7 us -> none  [the longest x3 6.49 us: contract(): lax.dot_general(segment, matrix_rows, (((1,), (1,)), ((), ())), precision...]
    all_to_all x1 -> x0, starting transfers between devices: 6.46 us -> none  [shards(): lax.all_to_all(outgoing, ('sub', 'grp'), split_axis=1, concat_axis=1, til...]
    all_to_all x1 -> x0, waiting for transfers between devices: 4.46 us -> none  [shards(): lax.all_to_all(outgoing, ('sub', 'grp'), split_axis=1, concat_axis=1, til...]
    ppermute x8 -> x0, starting transfers between devices: 4.03 us -> none  [shifted(): lax.ppermute(array, axis, [(i, (i + by) % count) for i in range(count)])]
  transfers between devices with their start and end apart: 9 -> 0, of which waited for: 9 -> 0; matrix products, arithmetic and copies ran while one was open for 2% -> 0% of each run, Pallas kernels for 0% -> 0%
where the time goes in v1:
time: 69.5 us; the launch traced here: 69 us
  Pallas kernels  60.4 us (87%)
  local copies, waits for them, and re-layouts  6.69 us (10%)
  other arithmetic  1.28 us (2%)
    pallas_call x1, Pallas kernels, shards(): pl.pallas_call(functools.partial(kernel, n, groups), out_shape=(jax.Shape...  60.4 us
    unnamed x5, local copies, waits for them, and re-layouts  6.69 us

profile of v1, /device:TPU:0, one launch (start us, length us, event | category | flops | bytes accessed | tf_op | source)
XLA Modules:
  0.0 69.0 jit_solution(8937834089017692909)
XLA Ops:
  0.6 1.3 %select_reduce_fusion.inverse = s32[32]{0:T(128)} fusion(s32[32]{0:T(128)} %param.19), kind=kLoop, calls=%fused_computation | loop fusion | flops 3040 | bytes 256 | tf_op jit(solution)/shard_map/reduce_sum | solution.py:407
  1.9 60.4 %shard_map.137 = (f32[8,2,512]{2,1,0:T(2,128)}, f32[8,2,512]{2,1,0:T(2,128)}, f32[8,256]{1,0:T(8,128)}, f32[8,8]{1,0:T(8,128)}, f32[8,1024]{1,0:T(8,128)}) custom-call(s32[32]{0:T(128)} %select_reduce_fusion.inverse, f32[2,512,512]{2,1,0:T(8,128)} %rr_hbm.1, f32[2,64,512]{2,1,0:T(8,128)} %modes_hbm.1, f32[64,2048]{1,0:T(8,128)} %coarse_hbm.1, ...), custom_call_target="tpu_custom_call" | custom-call | tf_op jit(solution)/shard_map/pallas_call | solution.py:414
  62.3 1.4 %copy.20 = f32[8,2,512]{2,1,0:T(2,128)} copy(f32[8,2,512]{2,1,0:T(2,128)} %get-tuple-element.20) | data formatting | bytes 65536
  63.7 1.4 %copy.21 = f32[8,2,512]{2,1,0:T(2,128)} copy(f32[8,2,512]{2,1,0:T(2,128)} %get-tuple-element.21) | data formatting | bytes 65536
  65.1 1.3 %copy.22 = f32[256,8]{0,1:T(8,128)} copy(f32[256,8]{0,1:T(8,128)} %bitcast.1) | data formatting | bytes 16384
  66.4 1.3 %copy.23 = f32[8,8]{1,0:T(8,128)} copy(f32[8,8]{1,0:T(8,128)} %get-tuple-element.23) | data formatting | bytes 512
  67.7 1.4 %copy.24 = f32[8,1024]{1,0:T(8,128)} copy(f32[8,1024]{1,0:T(8,128)} %get-tuple-element.24) | data formatting | bytes 65536

commit v2 on v1

--- a/solution.py
+++ b/solution.py
@@ -31,24 +31,68 @@
     )
 
 
+def split(x):
+    first = x.astype(jnp.bfloat16)
+    rest = x - first.astype(jnp.float32)
+    second = rest.astype(jnp.bfloat16)
+    return first, second, (rest - second.astype(jnp.float32)).astype(jnp.bfloat16)
+
+
+def keep_split(parts, matrix):
+    for at, part in enumerate(split(matrix)):
+        parts[at] = part
+
+
+def split_dot(x, parts, contracted):
+    first, second, third = split(x)
+    stacked = jnp.concatenate([first, second, third, jnp.zeros_like(first)], axis=0)
+    rows = x.shape[0]
+
+    def product(a, b):
+        return lax.dot_general(a, b, (((1,), (contracted,)), ((), ())), preferred_element_type=jnp.float32)
+
+    large = product(stacked, parts[0])
+    middle = product(stacked[: 2 * rows], parts[1])
+    small = product(stacked[: 2 * rows], parts[2])
+    correction = large[2 * rows : 3 * rows] + middle[rows : 2 * rows] + small[:rows]
+    return large[:rows] + (large[rows : 2 * rows] + middle[:rows] + correction)
+
+
+def hand_over(*refs):
+    half = len(refs) // 2
+    for source, target in zip(refs[:half], refs[half:]):
+        target[...] = source[...]
+
+
 def kernel(
     n,
     groups,
-    inverse,
+    inner,
+    owner_hbm,
     rr_hbm,
     modes_hbm,
     coarse_hbm,
     basis_hbm,
+    inertia_hbm,
+    disp_hbm,
+    vel_hbm,
+    acc_hbm,
+    load_hbm,
+    disp_out,
+    vel_out,
+    proj_out,
+    r_out,
+    cols_out,
+    owner,
+    inverse,
     inertia,
     disp_now,
     vel_now,
     acc_now,
     load_next,
-    disp_out,
-    vel_out,
-    proj_out,
-    r_out,
-    cols_out,
+    coarse_parts,
+    inter_parts,
+    basis_parts,
     rr,
     modes,
     coarse,
@@ -65,6 +109,7 @@
     outgoing,
     incoming,
     proj_parts,
+    proj_sums,
     gram_parts,
     green,
     local_sem,
@@ -103,7 +148,23 @@
     load_modes = pltpu.make_async_copy(modes_hbm, modes, local_sem.at[1])
     load_coarse = pltpu.make_async_copy(coarse_hbm, coarse.at[pl.ds(0, rows)], local_sem.at[2])
     load_basis = pltpu.make_async_copy(basis_hbm, basis, local_sem.at[3])
+    fields_in = [
+        pltpu.make_async_copy(source, target, local_sem.at[4 + at])
+        for at, (source, target) in enumerate(
+            (
+                (inertia_hbm, inertia),
+                (disp_hbm, disp_now),
+                (vel_hbm, vel_now),
+                (acc_hbm, acc_now),
+                (load_hbm, load_next),
+            )
+        )
+    ]
+    load_owner = pltpu.make_async_copy(owner_hbm, owner, local_sem.at[9])
     load_modes.start()
+    for copy in fields_in:
+        copy.start()
+    load_owner.start()
     load_rr.start()
     load_coarse.start()
     load_basis.start()
@@ -118,6 +179,8 @@
             + (0.5 - newmark_beta) * time_step * time_step * acc_now[:, k, :]
         )
 
+    for copy in fields_in:
+        copy.wait()
     sides = [right_side(k) for k in range(sub_count)]
 
     corner[...] = jnp.zeros_like(corner)
@@ -191,6 +254,19 @@
     inter[2 * NC : 3 * NC, NI:] = -modes_next[NC:, :]
     inter[3 * NC :, 0:NI] = modes[0, :NC, unknowns - NI :]
 
+    keep_split(inter_parts, inter[...])
+    keep_split(coarse_parts, coarse[...])
+    load_owner.wait()
+
+    def find(t, carry):
+        at = jnp.int32(0)
+        for p in range(n):
+            at = jnp.where(owner[p] == t, p, at)
+        inverse[t] = at
+        return carry
+
+    lax.fori_loop(0, n, find, 0)
+
     def coarse_solve(at):
         all_but_one(gathered, at, wide_recv.at[at]).wait()
         assembled = []
@@ -198,7 +274,7 @@
             low = jnp.where(lane < 96, gathered[at, 2 * j], gathered[at, (2 * j + 2) % n])
             high = jnp.where(lane >= 32, gathered[at, 2 * j + 1], gathered[at, (2 * j - 1) % n])
             assembled.append(low + high)
-        return nt(jnp.concatenate(assembled, axis=1), coarse[...])
+        return split_dot(jnp.concatenate(assembled, axis=1), coarse_parts, 1)
 
     def jumps(fields, next_first):
         firsts = [field[:, :NI] for field in fields[1:]] + [next_first]
@@ -223,13 +299,10 @@
 
     solved = coarse_solve(0)
     edges[0].wait_recv()
-    first_fields = [
-        local[k] + nn(solved, corner[:, k * unknowns : (k + 1) * unknowns]) for k in range(sub_count)
-    ]
-    vector0 = jumps(local, edge[0]) + nn(solved, inter[...])
+    vector0 = jumps(local, edge[0]) + split_dot(solved, inter_parts, 0)
 
     def start_image(vector, at):
-        gathered[at, me] = placed(nt(vector, inter[...]))
+        gathered[at, me] = placed(split_dot(vector, inter_parts, 1))
         broadcast(gathered, at, at)
         slot = 2 * at - 1
         edge_out[slot] = vector[:, NI:]
@@ -253,22 +326,25 @@
         edges[slot + 1].wait_recv()
         first = nn(-edge[slot], rr[0, :NI, :]) + nn(head, rr[0, unknowns - NI :, :])
         beyond = nn(-tail, rr_next[:NI, :]) + nn(edge[slot + 1], rr_next[NI:, :])
-        inner = [first, second]
+        inside = [first, second]
         values = coarse_solve(at)
-        fields = [
-            inner[k] + nn(values, corner[:, k * unknowns : (k + 1) * unknowns]) for k in range(sub_count)
+        return inside, values, jumps(inside, beyond) + split_dot(values, inter_parts, 0)
+
+    def with_corners(inside, values):
+        return [
+            inside[k] + nn(values, corner[:, k * unknowns : (k + 1) * unknowns]) for k in range(sub_count)
         ]
-        return fields, jumps(inner, beyond) + nn(values, inter[...])
 
     def column(values):
         return jnp.sum(values, axis=1, keepdims=True)
 
     start_image(vector0, 1)
+    first_fields = with_corners(local, solved)
     for k in range(sub_count):
         green[k] = first_fields[k]
     for p in range(n):
         pieces[p] = piece_part(first_fields, 0, p)
-    fields0, vector1 = end_image(vector0, 1)
+    inside0, values0, vector1 = end_image(vector0, 1)
 
     start_image(vector1, 2)
     norm_row = jnp.where(lane == sublane, column(vector0 * vector0), 0.0) + jnp.where(
@@ -276,9 +352,13 @@
     )
     norms[0, me] = jnp.sum(norm_row, axis=0, keepdims=True)
     broadcast(norms, 0, 3)
+    fields0 = with_corners(inside0, values0)
     for p in range(n):
         pieces[p] = pieces[p] + piece_part(fields0, 1, p)
-    fields1, vector2 = end_image(vector1, 2)
+    load_basis.wait()
+    keep_split(basis_parts, basis[...])
+    inside1, values1, vector2 = end_image(vector1, 2)
+    fields1 = with_corners(inside1, values1)
 
     all_but_one(norms, 0, wide_recv.at[3]).wait()
     totals = jnp.broadcast_to(jnp.sum(norms[0], axis=0), (8, LANES))
@@ -302,7 +382,6 @@
 
     others(send_piece)
     incoming[0, me] = outgoing[me]
-    load_basis.wait()
     all_but_one(incoming, 0, wide_recv.at[4]).wait()
 
     sums = jnp.sum(incoming[0], axis=0)
@@ -331,8 +410,12 @@
             tile = jnp.where((lane >= i * width) & (lane < (i + 1) * width), total, tile)
         snapshot_tiles.append(tile)
     snapshots = jnp.concatenate(snapshot_tiles, axis=1)
-    proj_parts[0, me] = nn(snapshots, basis[...])
-    broadcast(proj_parts, 0, 5)
+    plane, outer = me // inner, n // inner
+    seat = lax.rem(me, inner)
+    proj_parts[seat] = split_dot(snapshots, basis_parts, 0)
+    for i in range(1, inner):
+        rank = plane * inner + lax.rem(seat + i, inner)
+        remote(proj_parts.at[seat], proj_parts.at[seat], wide_send.at[5], wide_recv.at[5], rank).start()
 
     for k in range(sub_count):
         carried = green[k] - scale0 * fields0[k] - scale1 * fields1[k]
@@ -345,10 +428,19 @@
         disp_out[:, k, :] = carried
         vel_out[:, k, :] = vel + time_step * ((1.0 - newmark_gamma) * acc + newmark_gamma * accel_new)
 
-    all_but_one(proj_parts, 0, wide_recv.at[5]).wait()
-    projection = jnp.sum(proj_parts[0], axis=0)
+    pltpu.make_async_copy(
+        proj_parts.at[pl.ds(0, inner - 1)], proj_parts.at[pl.ds(0, inner - 1)], wide_recv.at[5]
+    ).wait()
+    proj_sums[plane] = jnp.sum(proj_parts[...], axis=0)
+    for i in range(1, outer):
+        rank = lax.rem(plane + i, outer) * inner + seat
+        remote(proj_sums.at[plane], proj_sums.at[plane], wide_send.at[7], wide_recv.at[7], rank).start()
+    pltpu.make_async_copy(
+        proj_sums.at[pl.ds(0, outer - 1)], proj_sums.at[pl.ds(0, outer - 1)], wide_recv.at[7]
+    ).wait()
+    projection = jnp.sum(proj_sums[...], axis=0)
     proj_out[...] = projection
-    remainder = snapshots - nt(projection, basis[...])
+    remainder = snapshots - split_dot(projection, basis_parts, 1)
     repeated = jnp.concatenate([remainder] * (LANES // 8), axis=0)
     gram_wide = nt(remainder, repeated)
     gram_parts[0, me] = jnp.sum(
@@ -380,13 +472,19 @@
         all_but_one(gathered, at, wide_send.at[at]).wait()
     all_but_one(norms, 0, wide_send.at[3]).wait()
     all_but_one(incoming, 0, wide_send.at[4]).wait()
-    all_but_one(proj_parts, 0, wide_send.at[5]).wait()
+    pltpu.make_async_copy(
+        proj_parts.at[pl.ds(0, inner - 1)], proj_parts.at[pl.ds(0, inner - 1)], wide_send.at[5]
+    ).wait()
+    pltpu.make_async_copy(
+        proj_sums.at[pl.ds(0, outer - 1)], proj_sums.at[pl.ds(0, outer - 1)], wide_send.at[7]
+    ).wait()
     all_but_one(gram_parts, 0, wide_send.at[6]).wait()
 
 
 def solution(mesh):
     groups = mesh.shape["grp"]
     n = mesh.shape["sub"] * groups
+    inner = math.gcd(n, 8)
 
     def shards(
         rr_inverse,
@@ -403,26 +501,33 @@
         case_count, sub_count, unknowns = disp_now.shape
         rank = basis_rows.shape[1]
         local_rows = basis_rows.shape[0]
-        counting = jnp.arange(n, dtype=jnp.int32)
-        inverse = jnp.sum(
-            jnp.where(piece_owner[None, :] == counting[:, None], counting[None, :], 0), axis=1, dtype=jnp.int32
-        )
         width = (sub_count + 2) * NC
         f32 = jnp.float32
         vmem = pl.BlockSpec(memory_space=pltpu.VMEM)
         anywhere = pl.BlockSpec(memory_space=pl.ANY)
-        disp, vel, proj, r_factor, columns = pl.pallas_call(
-            functools.partial(kernel, n, groups),
-            out_shape=(
-                jax.ShapeDtypeStruct(disp_now.shape, f32),
-                jax.ShapeDtypeStruct(disp_now.shape, f32),
-                jax.ShapeDtypeStruct((case_count, rank), f32),
-                jax.ShapeDtypeStruct((case_count, case_count), f32),
-                jax.ShapeDtypeStruct((case_count, local_rows), f32),
-            ),
-            in_specs=[pl.BlockSpec(memory_space=pltpu.SMEM)] + [anywhere] * 4 + [vmem] * 5,
+        results = (
+            jax.ShapeDtypeStruct(disp_now.shape, f32),
+            jax.ShapeDtypeStruct(disp_now.shape, f32),
+            jax.ShapeDtypeStruct((case_count, rank), f32),
+            jax.ShapeDtypeStruct((case_count, case_count), f32),
+            jax.ShapeDtypeStruct((case_count, local_rows), f32),
+        )
+        computed = pl.pallas_call(
+            functools.partial(kernel, n, groups, inner),
+            out_shape=results,
+            in_specs=[anywhere] * 10,
             out_specs=(vmem,) * 5,
             scratch_shapes=[
+                pltpu.SMEM(piece_owner.shape, jnp.int32),
+                pltpu.SMEM(piece_owner.shape, jnp.int32),
+                pltpu.VMEM(inertia.shape, f32),
+                pltpu.VMEM(disp_now.shape, f32),
+                pltpu.VMEM(vel_now.shape, f32),
+                pltpu.VMEM(acc_now.shape, f32),
+                pltpu.VMEM(load_next.shape, f32),
+                pltpu.VMEM((3, width, coarse_inverse.shape[1]), jnp.bfloat16),
+                pltpu.VMEM((3, width, sub_count * NI), jnp.bfloat16),
+                pltpu.VMEM((3,) + basis_rows.shape, jnp.bfloat16),
                 pltpu.VMEM(rr_inverse.shape, f32),
                 pltpu.VMEM(corner_modes.shape, f32),
                 pltpu.VMEM((width, coarse_inverse.shape[1]), f32),
@@ -438,20 +543,21 @@
                 pltpu.VMEM((n, case_count, LANES), f32),
                 pltpu.VMEM((n, case_count, LANES), f32),
                 pltpu.VMEM((1, n, case_count, LANES), f32),
-                pltpu.VMEM((1, n, case_count, rank), f32),
+                pltpu.VMEM((inner, case_count, rank), f32),
+                pltpu.VMEM((n // inner, case_count, rank), f32),
                 pltpu.VMEM((1, n, 1, LANES), f32),
                 pltpu.VMEM((sub_count, case_count, unknowns), f32),
-                pltpu.SemaphoreType.DMA((4,)),
+                pltpu.SemaphoreType.DMA((10,)),
                 pltpu.SemaphoreType.DMA((5,)),
                 pltpu.SemaphoreType.DMA((5,)),
-                pltpu.SemaphoreType.DMA((7,)),
-                pltpu.SemaphoreType.DMA((7,)),
+                pltpu.SemaphoreType.DMA((8,)),
+                pltpu.SemaphoreType.DMA((8,)),
                 pltpu.SemaphoreType.DMA((5,)),
                 pltpu.SemaphoreType.DMA((5,)),
             ],
             compiler_params=pltpu.CompilerParams(collective_id=0, has_side_effects=True),
         )(
-            inverse,
+            piece_owner,
             rr_inverse,
             corner_modes,
             coarse_inverse,
@@ -462,6 +568,9 @@
             acc_now,
             load_next,
         )
+        disp, vel, proj, r_factor, columns = pl.pallas_call(
+            hand_over, out_shape=results, in_specs=[vmem] * 5, out_specs=(vmem,) * 5
+        )(*computed)
         return disp, vel, proj.T, r_factor, columns
 
     return jax.shard_map(

time: 69.5 us -> 55.7 us (0.80)
  local copies, waits for them, and re-layouts: 6.69 us -> 0 us
  Pallas kernels: 60.4 us -> 54.9 us
  other arithmetic: 1.28 us -> 0 us
    unnamed x5 -> x0, local copies, waits for them, and re-layouts: 6.69 us -> none
    pallas_call x1 -> x2, Pallas kernels: 60.4 us -> 54.9 us  [the longest x1 53.4 us: shards(): pl.pallas_call(functools.partial(kernel, n, groups, inner), out_shape=res...]
    reduce_sum x1 -> x0, other arithmetic: 1.28 us -> none  [shards(): jnp.sum(jnp.where(piece_owner[None, :] == counting[:, None], counting[Non...]
where the time goes in v2:
time: 55.7 us; the launch traced here: 55.5 us
  Pallas kernels  54.9 us (99%)
  between operations  0.64 us (1%)
    pallas_call x1, Pallas kernels, shards(): pl.pallas_call(functools.partial(kernel, n, groups, inner), out_shape=res...  53.4 us
    pallas_call x1, Pallas kernels, shards(): pl.pallas_call(hand_over, out_shape=results, in_specs=[vmem] * 5, out_spe...  1.46 us

profile of v2, /device:TPU:0, one launch (start us, length us, event | category | flops | bytes accessed | tf_op | source)
XLA Modules:
  0.0 55.5 jit_solution(14557732303557705080)
XLA Ops:
  0.6 53.4 %shard_map.137 = (f32[8,2,512]{2,1,0:T(2,128)}, f32[8,2,512]{2,1,0:T(2,128)}, f32[8,256]{1,0:T(8,128)}, f32[8,8]{1,0:T(8,128)}, f32[8,1024]{1,0:T(8,128)}) custom-call(s32[32]{0:T(128)} %owner_hbm.1, f32[2,512,512]{2,1,0:T(8,128)} %rr_hbm.1, f32[2,64,512]{2,1,0:T(8,128)} %modes_hbm.1, f32[64,2048]{1,0:T(8,128)} %coarse_hbm.1, f32[1024,256]{1,0:T(8,128)} %basis_hbm.1, ...), custom_call_target="tpu_custom_call" | custom-call | tf_op jit(solution)/shard_map/pallas_call | solution.py:515
  54.1 1.5 %shard_map.138 = (f32[8,2,512]{2,1,0:T(2,128)}, f32[8,2,512]{2,1,0:T(2,128)}, f32[8,256]{1,0:T(8,128)}, f32[8,8]{1,0:T(8,128)}, f32[8,1024]{1,0:T(8,128)}) custom-call(f32[8,2,512]{2,1,0:T(2,128)} %get-tuple-element.15.refs_0_, f32[8,2,512]{2,1,0:T(2,128)} %get-tuple-element.16.refs_1_, f32[8,256]{1,0:T(8,128)} %get-tuple-element.17.refs_2_, ...), custom_call_target="tpu_custom_call" | custom-call | tf_op jit(solution)/shard_map/pallas_call | solution.py:571
